TPU v7x, 32 devices: a whole 2x2x4 slice. The times are simulated.
32 devices in a mesh: row: 8 (over z, y), col: 4 (over x, core).
Axes of the slice: x: 2, y: 2, z: 4, core: 2. Of those that a mesh axis runs over, the one named last changes fastest.
Arguments:
- dens_alpha: bfloat16 [2048, 2048], P('row', 'col'), may hold values from -6 to 6
- dens_beta: bfloat16 [2048, 2048], P('row', 'col'), may hold values from -6 to 6
- integrals: bfloat16 [512, 256, 256], P(('row', 'col')), may hold values from -0.375 to 0.375
- tile_quartet: int32 [512, 4], P(('row', 'col')), may hold values from 0 to 127, as said below
- tile_count: int32 [32], P(('row', 'col')), may hold values from 2 to 16, as said below
Outputs:
- fock_alpha: float32 [2048, 2048], P('row', 'col')
- fock_beta: float32 [2048, 2048], P('row', 'col')
Inputs may be any that keep to these rules, and one draw needn't show every extreme that they name: `tile_quartet`: slots d * 16 to d * 16 + 15 belong to device d = i * 4 + j (i its row index, j its col index). Each row holds block indices P, Q, R, S of 16 functions; Q lies in i * 16 up to but excluding (i + 1) * 16, and R in j * 32 up to but excluding (j + 1) * 32; S may be any block. Among the 16 slots of one device, exactly 2 have P in each range k * 16 up to but excluding (k + 1) * 16, and so exactly 4 in each range of width 2048 // 64; their order within the device is arbitrary. `tile_count`: the live slots of a device are its first ones; some device has all 16 live.
All inputs are finite; a program needn't handle non-finite values.
Results may differ from a plain program's by a relative error of at most 0.0026.
Values may be sent and summed in bfloat16 or wider, within the bound.
A program may use at most 128 MiB of HBM per device.

v0:
```python
import jax
import jax.numpy as jnp
from jax import lax
from jax.sharding import PartitionSpec as P

NBASIS = 2048
SHELL = 16
GROUP = 8


def contract(tile_data, coul_dens, alpha_dens, beta_dens, live_count):
    slot_count = tile_data.shape[0]
    empty_block = jnp.zeros((slot_count, SHELL, SHELL), jnp.float32)
    group_total = (live_count + GROUP - 1) // GROUP

    def step_group(number, partial_value):
        first_slot = number * GROUP
        tile_piece = lax.dynamic_slice_in_dim(tile_data, first_slot, GROUP, 0).reshape(
            GROUP, SHELL, SHELL, SHELL, SHELL
        )
        coul_piece = lax.dynamic_slice_in_dim(coul_dens, first_slot, GROUP, 0)
        alpha_piece = lax.dynamic_slice_in_dim(alpha_dens, first_slot, GROUP, 0)
        beta_piece = lax.dynamic_slice_in_dim(beta_dens, first_slot, GROUP, 0)
        coul_out = jnp.einsum(
            "tpqrs,tsr->tqp", tile_piece, coul_piece, preferred_element_type=jnp.float32
        )
        alpha_out = jnp.einsum(
            "tpqrs,tqs->tpr", tile_piece, alpha_piece, preferred_element_type=jnp.float32
        )
        beta_out = jnp.einsum(
            "tpqrs,tqs->tpr", tile_piece, beta_piece, preferred_element_type=jnp.float32
        )
        return (
            lax.dynamic_update_slice_in_dim(partial_value[0], coul_out, first_slot, 0),
            lax.dynamic_update_slice_in_dim(partial_value[1], alpha_out, first_slot, 0),
            lax.dynamic_update_slice_in_dim(partial_value[2], beta_out, first_slot, 0),
        )

    results = lax.fori_loop(0, group_total, step_group, (empty_block, empty_block, empty_block))
    live_mask = (jnp.arange(slot_count, dtype=jnp.int32) < live_count).astype(jnp.float32)[
        :, None, None
    ]
    return (results[0] * live_mask, results[1] * live_mask, results[2] * live_mask)


def bucket_slots(destination, owner_count):
    hot = (destination[:, None] == jnp.arange(owner_count, dtype=jnp.int32)[None, :]).astype(
        jnp.int32
    )
    before = jnp.cumsum(hot, 0) - hot
    rank = jnp.sum(before * hot, 1)
    capacity = destination.shape[0] // owner_count
    return (destination * capacity + rank, capacity)


def local(dens_alpha, dens_beta, integrals, tile_quartet, tile_count):
    rows_dev, cols_dev = dens_alpha.shape
    slot_count = integrals.shape[0]
    row_blocks = rows_dev // SHELL
    col_blocks = cols_dev // SHELL
    all_blocks = NBASIS // SHELL
    summed = (dens_alpha.astype(jnp.float32) + dens_beta.astype(jnp.float32)).astype(jnp.bfloat16)
    dens_cols = lax.all_gather(summed, "row", axis=0, tiled=True)
    rows_alpha, rows_beta = (
        lax.all_gather(dens_alpha, "col", axis=1, tiled=True),
        lax.all_gather(dens_beta, "col", axis=1, tiled=True),
    )
    index_p = tile_quartet[:, 0]
    index_q = tile_quartet[:, 1]
    index_r = tile_quartet[:, 2]
    index_s = tile_quartet[:, 3]
    local_q = index_q - lax.axis_index("row") * row_blocks
    local_r = index_r - lax.axis_index("col") * col_blocks
    coul_dens = dens_cols.reshape(all_blocks, SHELL, col_blocks, SHELL)[index_s, :, local_r, :]
    alpha_dens = rows_alpha.reshape(row_blocks, SHELL, all_blocks, SHELL)[local_q, :, index_s, :]
    beta_dens = rows_beta.reshape(row_blocks, SHELL, all_blocks, SHELL)[local_q, :, index_s, :]
    live_count = tile_count[0]
    coul_res, alpha_res, beta_res = contract(
        integrals, coul_dens, alpha_dens, beta_dens, live_count
    )
    offsets = jnp.arange(SHELL, dtype=jnp.int32)
    col_count = lax.axis_size("col")
    row_count = lax.axis_size("row")
    coul_target, coul_cap = bucket_slots(index_p // col_blocks, col_count)
    coul_send = (
        jnp.zeros((col_count * coul_cap, SHELL * SHELL), jnp.float32)
        .at[coul_target]
        .set(coul_res.reshape(slot_count, SHELL * SHELL))
        .reshape(col_count, coul_cap, SHELL * SHELL)
    )
    empty_place = jnp.zeros((col_count * coul_cap,), jnp.int32)
    coul_place = jnp.stack(
        [
            empty_place.at[coul_target].set(local_q).reshape(col_count, coul_cap),
            empty_place.at[coul_target].set(index_p % col_blocks).reshape(col_count, coul_cap),
        ],
        1,
    )
    coul_recv = lax.all_to_all(coul_send, "col", split_axis=0, concat_axis=0, tiled=True)
    coul_where = lax.all_to_all(coul_place, "col", split_axis=0, concat_axis=0, tiled=True)
    rows_q = coul_where[:, 0, :].reshape(-1)[:, None, None] * SHELL + offsets[None, :, None]
    cols_p = coul_where[:, 1, :].reshape(-1)[:, None, None] * SHELL + offsets[None, None, :]
    coulomb = (
        jnp.zeros((rows_dev, cols_dev), jnp.float32)
        .at[rows_q, cols_p]
        .add(coul_recv.reshape(-1, SHELL, SHELL))
    )
    exch_target, exch_cap = bucket_slots(index_p // row_blocks, row_count)
    both_spins = jnp.concatenate(
        [alpha_res.reshape(slot_count, SHELL * SHELL), beta_res.reshape(slot_count, SHELL * SHELL)],
        1,
    )
    exch_send = (
        jnp.zeros((row_count * exch_cap, 2 * SHELL * SHELL), jnp.float32)
        .at[exch_target]
        .set(both_spins)
        .reshape(row_count, exch_cap, 2 * SHELL * SHELL)
    )
    blank_place = jnp.zeros((row_count * exch_cap,), jnp.int32)
    exch_place = jnp.stack(
        [
            blank_place.at[exch_target].set(index_p % row_blocks).reshape(row_count, exch_cap),
            blank_place.at[exch_target].set(local_r).reshape(row_count, exch_cap),
        ],
        1,
    )
    exch_recv = lax.all_to_all(exch_send, "row", split_axis=0, concat_axis=0, tiled=True)
    exch_where = lax.all_to_all(exch_place, "row", split_axis=0, concat_axis=0, tiled=True)
    rows_p = exch_where[:, 0, :].reshape(-1)[:, None, None] * SHELL + offsets[None, :, None]
    cols_r = exch_where[:, 1, :].reshape(-1)[:, None, None] * SHELL + offsets[None, None, :]
    exch_blocks = exch_recv.reshape(-1, 2, SHELL, SHELL)
    empty_local = jnp.zeros((rows_dev, cols_dev), jnp.float32)
    exch_alpha = empty_local.at[rows_p, cols_r].add(exch_blocks[:, 0])
    exch_beta = empty_local.at[rows_p, cols_r].add(exch_blocks[:, 1])
    return (coulomb - exch_alpha, coulomb - exch_beta)


def solution(mesh):
    in_specs = (
        P("row", "col"),
        P("row", "col"),
        P(("row", "col"), None, None),
        P(("row", "col"), None),
        P(("row", "col")),
    )
    out_specs = (P("row", "col"), P("row", "col"))
    return jax.shard_map(local, mesh=mesh, in_specs=in_specs, out_specs=out_specs, check_vma=False)
```

profile of v0, /device:TPU:0, one launch (start us, length us, event | category | flops | bytes accessed | tf_op | source)
XLA Modules:
  0.0 345.5 jit_solution(8182528428126751973)
XLA Ops:
  7.2 0.7 all-gather.6.cloned.1.call-update
  7.9 0.7 all-gather.8.cloned.1.call-update
  8.7 1.8 add_convert_fusion
  10.5 0.8 fusion.44
  12.0 0.6 scatter_custom_fusion
  12.7 0.7 and_select_fusion.2
  14.7 4.2 %all-to-all-start = ((s32[4,2,4]{2,1,0:T(2,128)}), s32[4,2,4]{2,1,0:T(2,128)S(1)}, u32[]{:S(2)}, u32[]{:S(2)}) async-start(s32[4,2,4]{2,1,0:T(2,128)} %copy.17), calls=%async_computation | async-start | bytes 8192 | tf_op jit(solution)/shard_map/all_to_all | solution.py:100
  19.6 0.6 scatter_custom_fusion.4
  20.3 0.6 scatter_custom_fusion.3
  21.6 1.1 all-to-all-done
  22.7 6.3 %all-to-all-start.2 = ((s32[8,2,2]{2,1,0:T(2,128)}), s32[8,2,2]{2,1,0:T(2,128)S(1)}, u32[]{:S(2)}, u32[]{:S(2)}) async-start(s32[8,2,2]{2,1,0:T(2,128)} %copy.21), calls=%async_computation.2 | async-start | bytes 16384 | tf_op jit(solution)/shard_map/all_to_all | solution.py:128
  29.4 6.2 %all-to-all-done.2 = s32[8,2,2]{2,1,0:T(2,128)S(1)} async-done(((s32[8,2,2]{2,1,0:T(2,128)}), s32[8,2,2]{2,1,0:T(2,128)S(1)}, u32[]{:S(2)}, u32[]{:S(2)}) %all-to-all-start.2) | async-done | bytes 160 | tf_op jit(solution)/shard_map/all_to_all | solution.py:128
  36.2 1.5 fusion.11
  37.6 0.9 fusion.21
  38.5 9.2 %reshape.195 = bf16[16,16,128,16]{3,2,1,0:T(8,128)(2,1)} reshape(bf16[256,2048]{1,0:T(8,128)(2,1)} %all-gather.6.cloned.1.call-done) | data formatting | bytes 2097152 | tf_op jit(solution)/shard_map/reshape | solution.py:75
  47.7 13.7 %copy.19 = bf16[16,16,128,16]{3,1,2,0:T(8,128)(2,1)} copy(bf16[16,16,128,16]{3,2,1,0:T(8,128)(2,1)} %reshape.195) | data formatting | bytes 2097152 | tf_op jit(solution)/shard_map/reshape | solution.py:75
  61.4 23.2 %reshape.196 = bf16[16,16,128,16]{3,2,1,0:T(8,128)(2,1)} reshape(bf16[256,2048]{1,0:T(8,128)(2,1)} %all-gather.8.cloned.1.call-done) | data formatting | bytes 2097152 | tf_op jit(solution)/shard_map/reshape | solution.py:76
  84.6 13.7 %copy.20 = bf16[16,16,128,16]{3,1,2,0:T(8,128)(2,1)} copy(bf16[16,16,128,16]{3,2,1,0:T(8,128)(2,1)} %reshape.196) | data formatting | bytes 2097152 | tf_op jit(solution)/shard_map/reshape | solution.py:76
  98.3 4.0 %gather_fusion.1 = bf16[16,16,16]{2,1,0:T(8,128)(2,1)S(1)} fusion(bf16[16,16,128,16]{3,1,2,0:T(8,128)(2,1)} %copy.19, s32[16]{0:T(128)S(1)} %get-tuple-element.87), kind=kCustom, calls=%fused_computation.1 | custom fusion | bytes 16512 | tf_op jit(solution)/shard_map/gather | solution.py:75
  102.3 4.0 %gather_fusion.2 = bf16[16,16,16]{2,1,0:T(8,128)(2,1)S(1)} fusion(bf16[16,16,128,16]{3,1,2,0:T(8,128)(2,1)} %copy.20, s32[16]{0:T(128)S(1)} %get-tuple-element.87), kind=kCustom, calls=%fused_computation.2 | custom fusion | bytes 16512 | tf_op jit(solution)/shard_map/gather | solution.py:76
  106.3 17.9 %reshape.194 = bf16[128,16,32,16]{3,2,1,0:T(8,128)(2,1)} reshape(bf16[2048,512]{1,0:T(8,128)(2,1)} %all-gather.4.cloned.1.call-done) | data formatting | bytes 4194304 | tf_op jit(solution)/shard_map/reshape | solution.py:74
  124.2 17.7 %copy.18 = bf16[128,16,32,16]{3,1,2,0:T(8,128)(2,1)} copy(bf16[128,16,32,16]{3,2,1,0:T(8,128)(2,1)} %reshape.194) | data formatting | bytes 4194304 | tf_op jit(solution)/shard_map/reshape | solution.py:74
  141.8 6.4 %gather_fusion = bf16[16,16,16]{2,1,0:T(8,128)(2,1)S(1)} fusion(bf16[128,16,32,16]{3,1,2,0:T(8,128)(2,1)} %copy.18, s32[16]{0:T(128)S(1)} %get-tuple-element.91), kind=kCustom, calls=%fused_computation | custom fusion | bytes 16512 | tf_op jit(solution)/shard_map/gather | solution.py:74
  148.2 0.7 broadcast_in_dim.17
  148.9 0.7 broadcast_in_dim.17.clone
  149.5 0.6 broadcast_in_dim.17.clone.1
  150.2 87.7 %while.14 = (s32[]{:T(128)}, f32[16,16,16]{2,1,0:T(8,128)}, f32[16,16,16]{2,1,0:T(8,128)}, f32[16,16,16]{2,1,0:T(8,128)}, s32[]{:T(128)}, /*index=5*/bf16[16,16,...) while((s32[]{:T(128)}, f32[16,16,16]{2,1,0:T(8,128)}, ...), condition=%wide.region_5.6_spmd, body=%wide.region_4.5_spmd.sunk | while | flops 3670022 | bytes 8229227 | solution.py:39
  150.3 7.5 %reshape.352 = bf16[8,16,16,16,16]{4,3,2,1,0:T(8,128)(2,1)} reshape(bf16[8,256,256]{2,1,0:T(8,128)(2,1)S(1)} %constant_dynamic-slice_fusion.2) | data formatting | bytes 2097152 | tf_op jit(solution)/shard_map/while/body/reshape | solution.py:18
  157.9 8.8 %multiply_reduce_fusion.2 = f32[8,16,16]{2,1,0:T(8,128)S(1)} fusion(f32[8,16,16]{2,1,0:T(8,128)S(1)} %copy.47, bf16[8,16,16,16,16]{4,3,2,1,0:T(8,128)(2,1)} %reshape.352), kind=kLoop, calls=%fused_computation.12.clone.1 | loop fusion | flops 1570816 | bytes 1064960 | tf_op jit(solution)/shard_map/while
  166.8 13.2 %fusion.70 = f32[8,1,16,16,1]{3,1,4,2,0:T(1,128)S(1)} fusion(bf16[8,16,16,16,16]{4,3,2,1,0:T(8,128)(2,1)} %reshape.352, bf16[8,16,16,1,1]{2,1,0,3,4:T(8,128)(2,1)S(1)} %dynamic-slice_bitcast_fusion.4), kind=kOutput, calls=%fused_computation.14.clone.1 | convolution fusion | flops 1048576 | bytes 1060864 | tf_op jit(solution)/shard_map/while/body/tpqrs,tqs->tpr/dot_general | solution.py:30
  180.1 13.2 %fusion.71 = f32[8,1,16,16,1]{3,1,4,2,0:T(1,128)S(1)} fusion(bf16[8,16,16,16,16]{4,3,2,1,0:T(8,128)(2,1)} %reshape.352, bf16[8,16,16,1,1]{2,1,0,3,4:T(8,128)(2,1)S(1)} %dynamic-slice_bitcast_fusion.5), kind=kOutput, calls=%fused_computation.16.clone.1 | convolution fusion | flops 1048576 | bytes 1060864 | tf_op jit(solution)/shard_map/while/body/tpqrs,tqs->tpr/dot_general | solution.py:27
  194.1 7.5 %reshape.352 = bf16[8,16,16,16,16]{4,3,2,1,0:T(8,128)(2,1)} reshape(bf16[8,256,256]{2,1,0:T(8,128)(2,1)S(1)} %constant_dynamic-slice_fusion.2) | data formatting | bytes 2097152 | tf_op jit(solution)/shard_map/while/body/reshape | solution.py:18
  201.7 8.8 %multiply_reduce_fusion.2 = f32[8,16,16]{2,1,0:T(8,128)S(1)} fusion(f32[8,16,16]{2,1,0:T(8,128)S(1)} %copy.47, bf16[8,16,16,16,16]{4,3,2,1,0:T(8,128)(2,1)} %reshape.352), kind=kLoop, calls=%fused_computation.12.clone.1 | loop fusion | flops 1570816 | bytes 1064960 | tf_op jit(solution)/shard_map/while
  210.6 13.2 %fusion.70 = f32[8,1,16,16,1]{3,1,4,2,0:T(1,128)S(1)} fusion(bf16[8,16,16,16,16]{4,3,2,1,0:T(8,128)(2,1)} %reshape.352, bf16[8,16,16,1,1]{2,1,0,3,4:T(8,128)(2,1)S(1)} %dynamic-slice_bitcast_fusion.4), kind=kOutput, calls=%fused_computation.14.clone.1 | convolution fusion | flops 1048576 | bytes 1060864 | tf_op jit(solution)/shard_map/while/body/tpqrs,tqs->tpr/dot_general | solution.py:30
  223.9 13.2 %fusion.71 = f32[8,1,16,16,1]{3,1,4,2,0:T(1,128)S(1)} fusion(bf16[8,16,16,16,16]{4,3,2,1,0:T(8,128)(2,1)} %reshape.352, bf16[8,16,16,1,1]{2,1,0,3,4:T(8,128)(2,1)S(1)} %dynamic-slice_bitcast_fusion.5), kind=kOutput, calls=%fused_computation.16.clone.1 | convolution fusion | flops 1048576 | bytes 1060864 | tf_op jit(solution)/shard_map/while/body/tpqrs,tqs->tpr/dot_general | solution.py:27
  237.9 1.1 broadcast_multiply_fusion.1
  239.1 0.6 scatter_custom_fusion.2
  240.4 3.2 all-to-all-start.1
  243.6 0.9 broadcast_select_fusion
  244.8 0.7 scatter_custom_fusion.5
  245.4 0.6 reshape.202
  246.1 1.4 all-to-all-done.1
  247.4 3.3 all-to-all-start.3
  251.0 28.4 %scatter_custom_fusion.6 = f32[131072]{0:T(1024)S(1)} fusion(s32[4096]{0:T(1024)S(1)} %reshape.284, f32[4096]{0:T(1024)S(1)} %bitcast.82, f32[]{:T(128)} %constant.91.clone.1), kind=kCustom, calls=%fused_computation.39 | custom fusion | flops 4096 | bytes 524292
  279.9 28.4 %scatter_custom_fusion.7 = f32[131072]{0:T(1024)S(1)} fusion(s32[4096]{0:T(1024)S(1)} %reshape.290, f32[4096]{0:T(1024)S(1)} %reshape.292, f32[]{:T(128)} %constant.91.clone.1), kind=kCustom, calls=%fused_computation.37 | custom fusion | flops 4096 | bytes 524292
  308.3 28.4 %scatter_custom_fusion.8 = f32[131072]{0:T(1024)S(1)} fusion(s32[4096]{0:T(1024)S(1)} %reshape.290, f32[4096]{0:T(1024)S(1)} %reshape.298, f32[]{:T(128)} %constant.91.clone.1), kind=kCustom, calls=%fused_computation.35 | custom fusion | flops 4096 | bytes 524292
  336.8 0.9 reshape.216
  337.7 0.9 reshape.217
  (94 shorter events, 7.3 us)
Async XLA Ops:
  7.2 31.4 %all-gather.6.cloned.1.call-start = ((), (), s32[]{:S(2)}) async-start(), calls=%async_computation.5 | async-start | bytes 1310720 | tf_op jit(solution)/shard_map/all_gather | solution.py:65
  7.9 53.5 %all-gather.8.cloned.1.call-start = ((), (), s32[]{:S(2)}) async-start(), calls=%async_computation.6 | async-start | bytes 1310720 | tf_op jit(solution)/shard_map/all_gather | solution.py:66
  8.6 97.6 %all-gather.4.cloned.1.call-start = ((), (), s32[]{:S(2)}) async-start(), calls=%async_computation.4 | async-start | bytes 2359296 | tf_op jit(solution)/shard_map/all_gather | solution.py:63
  14.7 8.0 %all-to-all-start = ((s32[4,2,4]{2,1,0:T(2,128)}), s32[4,2,4]{2,1,0:T(2,128)S(1)}, u32[]{:S(2)}, u32[]{:S(2)}) async-start(s32[4,2,4]{2,1,0:T(2,128)} %copy.17), calls=%async_computation | async-start | bytes 8192 | tf_op jit(solution)/shard_map/all_to_all | solution.py:100
  22.7 12.9 %all-to-all-start.2 = ((s32[8,2,2]{2,1,0:T(2,128)}), s32[8,2,2]{2,1,0:T(2,128)S(1)}, u32[]{:S(2)}, u32[]{:S(2)}) async-start(s32[8,2,2]{2,1,0:T(2,128)} %copy.21), calls=%async_computation.2 | async-start | bytes 16384 | tf_op jit(solution)/shard_map/all_to_all | solution.py:128
  124.2 26.0 %copy-start = (bf16[16,256,256]{2,1,0:T(8,128)(2,1)S(1)}, bf16[16,256,256]{2,1,0:T(8,128)(2,1)}, u32[]{:S(2)}) copy-start(bf16[16,256,256]{2,1,0:T(8,128)(2,1)} %param.9) | copy-start | bytes 6291460
  157.9 22.1 %copy-start.1 = (f32[16,16,16]{2,1,0:T(8,128)S(1)}, f32[16,16,16]{2,1,0:T(8,128)}, u32[]{:S(2)}) copy-start(f32[16,16,16]{2,1,0:T(8,128)} %get-tuple-element.174) | copy-start | bytes 49156 | tf_op jit(solution)/shard_map/while
  157.9 22.1 %copy-start.5 = (f32[16,16,16]{2,1,0:T(8,128)S(1)}, f32[16,16,16]{2,1,0:T(8,128)}, u32[]{:S(2)}) copy-start(f32[16,16,16]{2,1,0:T(8,128)} %get-tuple-element.176) | copy-start | bytes 49156 | tf_op jit(solution)/shard_map/while
  166.8 26.6 %copy-start.3 = (f32[16,16,16]{2,1,0:T(8,128)S(1)}, f32[16,16,16]{2,1,0:T(8,128)}, u32[]{:S(2)}) copy-start(f32[16,16,16]{2,1,0:T(8,128)} %get-tuple-element.175) | copy-start | bytes 49156 | tf_op jit(solution)/shard_map/while
  180.0 13.3 %copy-start.2 = (f32[16,16,16]{2,1,0:T(8,128)}, f32[16,16,16]{2,1,0:T(8,128)S(1)}, u32[]{:S(2)}) copy-start(f32[16,16,16]{2,1,0:T(8,128)S(1)} %get-tuple-element.187) | copy-start | bytes 49156 | tf_op jit(solution)/shard_map/while
  180.1 13.3 %copy-start.6 = (f32[16,16,16]{2,1,0:T(8,128)}, f32[16,16,16]{2,1,0:T(8,128)S(1)}, u32[]{:S(2)}) copy-start(f32[16,16,16]{2,1,0:T(8,128)S(1)} %get-tuple-element.189) | copy-start | bytes 49156 | tf_op jit(solution)/shard_map/while
  193.4 0.7 copy-start.4
  201.7 22.1 %copy-start.1 = (f32[16,16,16]{2,1,0:T(8,128)S(1)}, f32[16,16,16]{2,1,0:T(8,128)}, u32[]{:S(2)}) copy-start(f32[16,16,16]{2,1,0:T(8,128)} %get-tuple-element.174) | copy-start | bytes 49156 | tf_op jit(solution)/shard_map/while
  201.7 22.1 %copy-start.5 = (f32[16,16,16]{2,1,0:T(8,128)S(1)}, f32[16,16,16]{2,1,0:T(8,128)}, u32[]{:S(2)}) copy-start(f32[16,16,16]{2,1,0:T(8,128)} %get-tuple-element.176) | copy-start | bytes 49156 | tf_op jit(solution)/shard_map/while
  210.6 26.6 %copy-start.3 = (f32[16,16,16]{2,1,0:T(8,128)S(1)}, f32[16,16,16]{2,1,0:T(8,128)}, u32[]{:S(2)}) copy-start(f32[16,16,16]{2,1,0:T(8,128)} %get-tuple-element.175) | copy-start | bytes 49156 | tf_op jit(solution)/shard_map/while
  223.9 13.3 %copy-start.2 = (f32[16,16,16]{2,1,0:T(8,128)}, f32[16,16,16]{2,1,0:T(8,128)S(1)}, u32[]{:S(2)}) copy-start(f32[16,16,16]{2,1,0:T(8,128)S(1)} %get-tuple-element.187) | copy-start | bytes 49156 | tf_op jit(solution)/shard_map/while
  223.9 13.3 %copy-start.6 = (f32[16,16,16]{2,1,0:T(8,128)}, f32[16,16,16]{2,1,0:T(8,128)S(1)}, u32[]{:S(2)}) copy-start(f32[16,16,16]{2,1,0:T(8,128)S(1)} %get-tuple-element.189) | copy-start | bytes 49156 | tf_op jit(solution)/shard_map/while
  237.2 0.7 copy-start.4
  240.4 7.1 %all-to-all-start.1 = ((f32[4,4,256]{2,1,0:T(4,128)}), f32[4,4,256]{2,1,0:T(4,128)S(1)}, u32[]{:S(2)}, u32[]{:S(2)}) async-start(f32[4,4,256]{2,1,0:T(4,128)} %reshape.198), calls=%async_computation.1 | async-start | bytes 32768 | tf_op jit(solution)/shard_map/all_to_all | solution.py:99
  247.4 32.0 %all-to-all-start.3 = ((f32[8,2,512]{2,1,0:T(2,128)}), f32[8,2,512]{2,1,0:T(2,128)S(1)}, u32[]{:S(2)}, u32[]{:S(2)}) async-start(f32[8,2,512]{2,1,0:T(2,128)} %reshape.202), calls=%async_computation.3 | async-start | bytes 65536 | tf_op jit(solution)/shard_map/all_to_all | solution.py:127
Sparse Core Ops, SparseCore 0:
  9.5 19.4 all-gather.5
  30.6 16.6 all-gather.7
  50.0 49.0 all-gather.3
where the time goes:
time: 351 us; the launch traced here: 345 us
  local copies, waits for them, and re-layouts  138 us (39%)
  other arithmetic  112 us (32%)
  matrix products  52.9 us (15%)
  starting transfers between devices  17.3 us (5%)
  between operations  15.1 us (4%)
  waiting for transfers between devices  10.1 us (3%)
    unnamed x7, other arithmetic  88.5 us
    reshape x2, local copies, waits for them, and re-layouts, local(): rows_beta.reshape(row_blocks, SHELL, all_blocks, SHELL)  36.9 us
    reshape x2, local copies, waits for them, and re-layouts, local(): dens_cols.reshape(all_blocks, SHELL, col_blocks, SHELL)  35.6 us
    dot_general x2, matrix products, step_group(): jnp.einsum('tpqrs,tqs->tpr', tile_piece, alpha_piece, preferred_element_t...  26.5 us
    dot_general x2, matrix products, step_group(): jnp.einsum('tpqrs,tqs->tpr', tile_piece, beta_piece, preferred_element_ty...  26.4 us
    reshape x2, local copies, waits for them, and re-layouts, local(): rows_alpha.reshape(row_blocks, SHELL, all_blocks, SHELL)  22.8 us
    while x4, other arithmetic  17.5 us
    reshape x2, local copies, waits for them, and re-layouts, step_group(): lax.dynamic_slice_in_dim(tile_data, first_slot, GROUP, 0)  15.1 us
  transfers between devices with their start and end apart: 7, of which 3 were waited for; matrix products, arithmetic and copies ran while one was open for 32% of the time, Pallas kernels for 0%

commit v1 on v0

v1 whole, which is shorter than its diff:
```python
import functools

import jax
import jax.numpy as jnp
from jax import lax
from jax.experimental import pallas as pl
from jax.experimental.pallas import tpu as pltpu
from jax.sharding import PartitionSpec as P

SHELL = 16
LANES = 128
PACK = LANES // SHELL
WORDS = 8
MESH = pl.DeviceIdType.MESH
F32 = jnp.float32
BF16 = jnp.bfloat16


def iota(shape, axis):
    return lax.broadcasted_iota(jnp.int32, shape, axis)


def one_hot(shape, test):
    return jnp.where(test(iota(shape, 0), iota(shape, 1)), 1.0, 0.0).astype(BF16)


def dot(left, right):
    return jnp.dot(left, right, preferred_element_type=F32)


def dot_split(value, right):
    high = value.astype(BF16)
    low = (value - high.astype(F32)).astype(BF16)
    return dot(high, right) + dot(low, right)


def build_kernel(
    n_row, n_col, quartet, count, dens_a, dens_b, tiles,
    out_x, out_c, place,
    meta_c, meta_r, split_a, split_b, summed, held, send_c, recv_c, send_r, recv_r,
    drep_a, drep_b, left_j, part_a, part_b, part_j,
    xs, xr, cs, cr,
    tile_sem, sems_c, semr_c, sems_r, semr_r,
):
    slots, width = tiles.shape[0], tiles.shape[1]
    row_blocks = dens_a.shape[0] // SHELL
    col_blocks = dens_a.shape[1] // SHELL
    chunks = col_blocks // PACK
    row_cap, col_cap = slots // n_row, slots // n_col
    my_row, my_col = lax.axis_index("row"), lax.axis_index("col")
    first_row, first_col = my_row * row_blocks, my_col * col_blocks

    def row_peer(step):
        return lax.rem(my_row + step, n_row)

    def col_peer(step):
        return lax.rem(my_col + step, n_col)

    def column_copy(kind, src, dst, peer, source):
        return pltpu.make_async_remote_copy(
            src_ref=src, dst_ref=dst,
            send_sem=sems_c.at[kind, peer], recv_sem=semr_c.at[kind, source],
            device_id=(peer, my_col), device_id_type=MESH,
        )

    def row_copy(kind, src, dst, peer, source):
        return pltpu.make_async_remote_copy(
            src_ref=src, dst_ref=dst,
            send_sem=sems_r.at[kind, peer], recv_sem=semr_r.at[kind, source],
            device_id=(my_row, peer), device_id_type=MESH,
        )

    barrier = pltpu.get_barrier_semaphore()
    for step in range(1, n_row):
        pl.semaphore_signal(
            barrier, inc=1, device_id=(row_peer(step), my_col), device_id_type=MESH
        )
    for step in range(1, n_col):
        pl.semaphore_signal(
            barrier, inc=1, device_id=(my_row, col_peer(step)), device_id_type=MESH
        )
    pieces = tile_sem.shape[0]
    piece = slots // pieces
    tile_copies = [
        pltpu.make_async_copy(
            tiles.at[pl.ds(n * piece, piece)], held.at[pl.ds(n * piece, piece)], tile_sem.at[n]
        )
        for n in range(pieces)
    ]
    for copy in tile_copies:
        copy.start()

    live_count = count[0]
    keys = [lax.div(quartet[t, 0], row_blocks) * slots + t for t in range(slots)]

    def pick(u, previous):
        found = [jnp.where(key > previous, key, 1 << 30) for key in keys]
        while len(found) > 1:
            found = [jnp.minimum(a, b) for a, b in zip(found[::2], found[1::2])]
        t = lax.rem(found[0], slots)
        words = [quartet[t, n] for n in range(4)] + [jnp.where(t < live_count, 1, 0), t]
        for n, word in enumerate(words):
            meta_c[my_row, u * WORDS + n] = word
            meta_r[my_col, u * WORDS + n] = word
        return found[0]

    lax.fori_loop(0, slots, pick, jnp.int32(-1))
    for block_row in range(row_blocks):
        for chunk in range(chunks):
            rows = slice(block_row * SHELL, (block_row + 1) * SHELL)
            lanes = slice(chunk * LANES, (chunk + 1) * LANES)
            alpha, beta = dens_a[rows, lanes], dens_b[rows, lanes]
            at = block_row * chunks + chunk
            split_a[at], split_b[at] = alpha, beta
            summed[at] = (alpha.astype(F32) + beta.astype(F32)).astype(BF16)

    pl.semaphore_wait(barrier, n_row + n_col - 2)
    for step in range(n_row - 1, 0, -1):
        column_copy(0, meta_c.at[my_row], meta_c.at[my_row], row_peer(step), my_row).start()
    for step in range(1, n_col):
        row_copy(0, meta_r.at[my_col], meta_r.at[my_col], col_peer(step), my_col).start()

    group = iota((SHELL, LANES), 1) // SHELL

    fold_one = one_hot((LANES, LANES), lambda i, j: lax.rem(i, SHELL) == lax.rem(j, SHELL))

    def block_of(ref, block_row, block_col, mine):
        chunk = ref[block_row * chunks + lax.div(block_col, PACK)].astype(F32)
        inside = jnp.where(mine, lax.rem(block_col, PACK), -1)
        return jnp.where(group == inside, chunk, 0.0)

    def packed_blocks(blocks):
        spread_out = dot(jnp.concatenate(blocks, axis=0).astype(BF16), fold_one)
        halves = []
        for half in range(slots // PACK):
            total = jnp.zeros((SHELL, LANES), F32)
            for slot in range(PACK):
                first = (half * PACK + slot) * SHELL
                total = jnp.where(group == slot, spread_out[first : first + SHELL], total)
            halves.append(total)
        return jnp.concatenate(halves, axis=0).astype(BF16)

    def answer_column(source, target):
        blocks = []
        for slot in range(slots):
            s_at = meta_c[source, slot * WORDS + 3] - first_row
            r_at = jnp.clip(meta_c[source, slot * WORDS + 2] - first_col, 0, col_blocks - 1)
            mine = (s_at >= 0) & (s_at < row_blocks)
            blocks.append(block_of(summed, jnp.where(mine, s_at, 0), r_at, mine))
        target[source] = packed_blocks(blocks)

    def answer_row(source, target):
        blocks = [[], []]
        for slot in range(slots):
            q_at = jnp.clip(meta_r[source, slot * WORDS + 1] - first_row, 0, row_blocks - 1)
            s_at = meta_r[source, slot * WORDS + 3] - first_col
            mine = (s_at >= 0) & (s_at < col_blocks)
            s_at = jnp.where(mine, s_at, 0)
            for x, ref in enumerate((split_a, split_b)):
                blocks[x].append(block_of(ref, q_at, s_at, mine))
        half_rows = slots // PACK * SHELL
        for x in range(2):
            target[source, x * half_rows : (x + 1) * half_rows, :] = packed_blocks(blocks[x])

    answer_column(my_row, recv_c)
    answer_row(my_col, recv_r)

    def serve_row(step, carry):
        peer = col_peer(step)
        row_copy(0, meta_r.at[peer], meta_r.at[peer], peer, peer).wait_recv()
        answer_row(peer, send_r)
        row_copy(1, send_r.at[peer], recv_r.at[my_col], peer, my_col).start()
        return carry

    def serve_column(step, carry):
        peer = row_peer(step)
        column_copy(0, meta_c.at[peer], meta_c.at[peer], peer, peer).wait_recv()
        answer_column(peer, send_c)
        column_copy(1, send_c.at[peer], recv_c.at[my_row], peer, my_row).start()
        return carry

    lax.fori_loop(1, n_col, serve_row, 0)
    lax.fori_loop(1, n_row, serve_column, 0)

    def place_row(source, carry):
        for m in range(row_cap):
            base = (my_row * row_cap + m) * WORDS
            at = (source * row_cap + m) * 4
            place[at] = meta_c[source, base] - first_row
            place[at + 1] = meta_c[source, base + 2] - first_col
            place[at + 2] = meta_c[source, base + 4]
        return carry

    def place_col(source, carry):
        for m in range(col_cap):
            base = (my_col * col_cap + m) * WORDS
            at = (slots + source * col_cap + m) * 4
            place[at] = meta_r[source, base + 1] - first_row
            place[at + 1] = meta_r[source, base] - first_col
            place[at + 2] = meta_r[source, base + 4]
        return carry

    lax.fori_loop(0, n_row, place_row, 0)
    lax.fori_loop(0, n_col, place_col, 0)

    fold = one_hot((LANES, width), lambda i, j: lax.rem(i, SHELL) == lax.rem(j, SHELL))
    spread = one_hot((LANES, width), lambda i, j: lax.rem(i, SHELL) == lax.div(j, SHELL))
    gather = one_hot((width, LANES), lambda i, j: lax.div(i, SHELL) == lax.rem(j, SHELL))
    total_rows = slots * SHELL
    same_slot = one_hot(
        (total_rows, total_rows), lambda i, j: lax.div(i, SHELL) == lax.div(j, SHELL)
    )
    shape = (total_rows, width)
    diagonal = lax.rem(iota(shape, 0), SHELL) == lax.rem(iota(shape, 1), SHELL)

    def expand(packed):
        return jnp.concatenate(
            [
                jnp.where(
                    group == t % PACK,
                    packed[(t // PACK) * SHELL : (t // PACK + 1) * SHELL],
                    0.0,
                )
                for t in range(slots)
            ],
            axis=0,
        ).astype(BF16)

    def arrive(count_of, copy_of, peer_of, ref):
        def wait(step, carry):
            copy_of(1, ref.at[peer_of(step)], ref.at[peer_of(step)], peer_of(step), peer_of(step)).wait_recv()
            return carry

        lax.fori_loop(1, count_of, wait, 0)
        total = ref[0].astype(F32)
        for n in range(1, count_of):
            total = total + ref[n].astype(F32)
        return total

    spins = arrive(n_col, row_copy, col_peer, recv_r)
    half_rows = (slots // PACK) * SHELL
    drep_a[...] = dot(expand(spins[:half_rows]), fold)
    drep_b[...] = dot(expand(spins[half_rows:]), fold)
    for copy in tile_copies:
        copy.wait()

    def exchange(t, carry):
        rows = pl.ds(pl.multiple_of(t * SHELL, SHELL), SHELL)
        tile = held[meta_c[my_row, t * WORDS + 5]].astype(F32).reshape(SHELL, SHELL, width)
        part_a[rows, :] = jnp.sum(tile * drep_a[rows, :][None], axis=1)
        part_b[rows, :] = jnp.sum(tile * drep_b[rows, :][None], axis=1)
        return carry

    lax.fori_loop(0, slots, exchange, 0)
    exch_a = dot_split(part_a[...], gather)
    exch_b = dot_split(part_b[...], gather)
    for k in range(n_row):
        total = jnp.zeros((SHELL, LANES), F32)
        for m in range(row_cap):
            first = (k * row_cap + m) * SHELL
            total = jnp.where(group == 2 * m, exch_a[first : first + SHELL], total)
            total = jnp.where(group == 2 * m + 1, exch_b[first : first + SHELL], total)
        xs[k] = total

    def send_x(step, carry):
        peer = row_peer(step)
        column_copy(2, xs.at[peer], xr.at[my_row], peer, my_row).start()
        return carry

    lax.fori_loop(1, n_row, send_x, 0)
    xr[my_row] = xs[my_row]

    coul = arrive(n_row, column_copy, row_peer, recv_c)
    left_j[...] = dot(
        same_slot, jnp.where(diagonal, dot(expand(coul), spread), 0.0).astype(BF16)
    ).astype(BF16)

    def coulomb(t, carry):
        rows = pl.ds(pl.multiple_of(t * SHELL, SHELL), SHELL)
        part_j[rows, :] = lax.dot_general(
            left_j[rows, :], held[meta_c[my_row, t * WORDS + 5]], (((1,), (1,)), ((), ())), preferred_element_type=F32
        )
        return carry

    lax.fori_loop(0, slots, coulomb, 0)
    coul_blocks = dot_split(jnp.where(diagonal, part_j[...], 0.0), gather)
    for k in range(n_col):
        total = jnp.zeros((SHELL, LANES), F32)
        for m in range(col_cap):
            first = (k * col_cap + m) * SHELL
            total = jnp.where(group == m, coul_blocks[first : first + SHELL], total)
        cs[k] = total

    def send_j(step, carry):
        peer = col_peer(step)
        row_copy(2, cs.at[peer], cr.at[my_col], peer, my_col).start()
        return carry

    lax.fori_loop(1, n_col, send_j, 0)
    cr[my_col] = cs[my_col]

    def finish_row(step, carry):
        peer = col_peer(step)
        row_copy(2, cs.at[peer], cr.at[peer], peer, peer).wait()
        row_copy(1, send_r.at[peer], recv_r.at[peer], peer, peer).wait_send()
        row_copy(0, meta_r.at[my_col], meta_r.at[my_col], peer, peer).wait_send()
        return carry

    def finish_column(step, carry):
        peer = row_peer(step)
        column_copy(2, xs.at[peer], xr.at[peer], peer, peer).wait()
        column_copy(1, send_c.at[peer], recv_c.at[peer], peer, peer).wait_send()
        column_copy(0, meta_c.at[my_row], meta_c.at[my_row], peer, peer).wait_send()
        return carry

    lax.fori_loop(1, n_row, finish_column, 0)
    lax.fori_loop(1, n_col, finish_row, 0)
    out_x[...] = xr[...]
    out_c[...] = cr[...]


def place_kernel(place, in_x, in_c, out_a, out_b):
    n_row, n_col = in_x.shape[0], in_c.shape[0]
    slots = place.shape[0] // 8
    row_cap, col_cap = slots // n_row, slots // n_col
    out_a[...] = jnp.zeros_like(out_a)
    out_b[...] = jnp.zeros_like(out_b)
    group = iota((SHELL, LANES), 1) // SHELL

    def where_to(at):
        block_col = place[at + 1]
        rows = pl.ds(pl.multiple_of(place[at] * SHELL, SHELL), SHELL)
        lanes = pl.ds(pl.multiple_of(lax.div(block_col, PACK) * LANES, LANES), LANES)
        inside = lax.rem(block_col, PACK)
        return rows, lanes, inside, group == jnp.where(place[at + 2] != 0, inside, -1)

    def moved(block, here, inside, mask):
        shift = lax.rem(inside - here + PACK, PACK) * SHELL
        return jnp.where(mask, pltpu.roll(block, shift, 1), 0.0)

    for source in range(n_col):
        block = in_c[source]
        for m in range(col_cap):
            rows, lanes, inside, mask = where_to((slots + source * col_cap + m) * 4)
            value = moved(block, m, inside, mask)
            out_a[rows, lanes] += value
            out_b[rows, lanes] += value
    for source in range(n_row):
        block = in_x[source]
        for m in range(row_cap):
            rows, lanes, inside, mask = where_to((source * row_cap + m) * 4)
            out_a[rows, lanes] -= moved(block, 2 * m, inside, mask)
            out_b[rows, lanes] -= moved(block, 2 * m + 1, inside, mask)


def local(n_row, n_col, dens_alpha, dens_beta, integrals, tile_quartet, tile_count):
    slots, width = integrals.shape[0], integrals.shape[1]
    vmem = pl.BlockSpec(memory_space=pltpu.VMEM)
    smem = pl.BlockSpec(memory_space=pltpu.SMEM)
    rows = slots * SHELL
    pack_rows = slots // PACK * SHELL
    meta_words = max(LANES, slots * WORDS)
    split = pltpu.VMEM((dens_alpha.size // (SHELL * LANES), SHELL, LANES), BF16)
    blocks_x, blocks_c, place = pl.pallas_call(
        functools.partial(build_kernel, n_row, n_col),
        out_shape=(
            jax.ShapeDtypeStruct((n_row, SHELL, LANES), F32),
            jax.ShapeDtypeStruct((n_col, SHELL, LANES), F32),
            jax.ShapeDtypeStruct((slots * 8,), jnp.int32),
        ),
        in_specs=[smem, smem, vmem, vmem, pl.BlockSpec(memory_space=pl.ANY)],
        out_specs=(vmem, vmem, smem),
        scratch_shapes=[
            pltpu.SMEM((n_row, meta_words), jnp.int32),
            pltpu.SMEM((n_col, meta_words), jnp.int32),
            split,
            split,
            split,
            pltpu.VMEM(integrals.shape, BF16),
            pltpu.VMEM((n_row, pack_rows, LANES), BF16),
            pltpu.VMEM((n_row, pack_rows, LANES), BF16),
            pltpu.VMEM((n_col, 2 * pack_rows, LANES), BF16),
            pltpu.VMEM((n_col, 2 * pack_rows, LANES), BF16),
            pltpu.VMEM((rows, width), F32),
            pltpu.VMEM((rows, width), F32),
            pltpu.VMEM((rows, width), BF16),
            pltpu.VMEM((rows, width), F32),
            pltpu.VMEM((rows, width), F32),
            pltpu.VMEM((rows, width), F32),
            pltpu.VMEM((n_row, SHELL, LANES), F32),
            pltpu.VMEM((n_row, SHELL, LANES), F32),
            pltpu.VMEM((n_col, SHELL, LANES), F32),
            pltpu.VMEM((n_col, SHELL, LANES), F32),
            pltpu.SemaphoreType.DMA((4,)),
            pltpu.SemaphoreType.DMA((3, n_row)),
            pltpu.SemaphoreType.DMA((3, n_row)),
            pltpu.SemaphoreType.DMA((3, n_col)),
            pltpu.SemaphoreType.DMA((3, n_col)),
        ],
        compiler_params=pltpu.CompilerParams(collective_id=0, has_side_effects=True),
        name="build",
    )(tile_quartet, tile_count, dens_alpha, dens_beta, integrals)
    out = jax.ShapeDtypeStruct(dens_alpha.shape, F32)
    return pl.pallas_call(
        place_kernel,
        out_shape=(out, out),
        in_specs=[smem, vmem, vmem],
        out_specs=(vmem, vmem),
        name="place",
    )(place, blocks_x, blocks_c)


def solution(mesh):
    in_specs = (
        P("row", "col"),
        P("row", "col"),
        P(("row", "col"), None, None),
        P(("row", "col"), None),
        P(("row", "col")),
    )
    body = functools.partial(local, mesh.shape["row"], mesh.shape["col"])
    return jax.shard_map(
        body, mesh=mesh, in_specs=in_specs, out_specs=(P("row", "col"), P("row", "col")),
        check_vma=False,
    )
```

time: 351 us -> 28.6 us (0.08); the launches traced: 345 us -> 28.4 us
  local copies, waits for them, and re-layouts: 138 us -> 1.36 us
  other arithmetic: 112 us -> 0 us
  matrix products: 52.9 us -> 0 us
  Pallas kernels: 0 us -> 25.7 us
  starting transfers between devices: 17.3 us -> 0 us
  between operations: 15.1 us -> 1.29 us
  waiting for transfers between devices: 10.1 us -> 0 us
    reshape x14 -> x0, local copies, waits for them, and re-layouts: 112 us -> none  [the longest x2 36.9 us: local(): rows_beta.reshape(row_blocks, SHELL, all_blocks, SHELL)]
    unnamed x7 -> x0, other arithmetic: 88.5 us -> none
    dot_general x4 -> x0, matrix products: 52.9 us -> none  [the longest x2 26.5 us: step_group(): jnp.einsum('tpqrs,tqs->tpr', tile_piece, alpha_piece, preferred_element_t...]
    pallas_call x0 -> x2, Pallas kernels: none -> 25.7 us  [the longest x1 23.6 us: local(): pl.pallas_call(functools.partial(build_kernel, n_row, n_col), out_shape=(...]
    while x4 -> x0, other arithmetic: 17.5 us -> none
    all_to_all x4 -> x0, starting transfers between devices: 17.2 us -> none  [the longest x1 6.35 us: local(): lax.all_to_all(exch_place, 'row', split_axis=0, concat_axis=0, tiled=True)]
    gather x3 -> x0, local copies, waits for them, and re-layouts: 14.3 us -> none  [the longest x1 6.37 us: local(): dens_cols.reshape(all_blocks, SHELL, col_blocks, SHELL)]
    all_to_all x4 -> x0, waiting for transfers between devices: 8.64 us -> none  [the longest x1 6.18 us: local(): lax.all_to_all(exch_place, 'row', split_axis=0, concat_axis=0, tiled=True)]
  transfers between devices with their start and end apart: 7 -> 0, of which waited for: 3 -> 0; matrix products, arithmetic and copies ran while one was open for 32% -> 0% of each run, Pallas kernels for 0% -> 0%
where the time goes in v1:
time: 28.6 us; the launch traced here: 28.4 us
  Pallas kernels  25.7 us (90%)
  local copies, waits for them, and re-layouts  1.36 us (5%)
  between operations  1.29 us (5%)
    pallas_call x1, Pallas kernels, local(): pl.pallas_call(functools.partial(build_kernel, n_row, n_col), out_shape=(...  23.6 us
    pallas_call x1, Pallas kernels, local(): pl.pallas_call(place_kernel, out_shape=(out, out), in_specs=[smem, vmem,...  2.16 us
    unnamed x1, local copies, waits for them, and re-layouts  1.36 us

profile of v1, /device:TPU:0, one launch (start us, length us, event | category | flops | bytes accessed | tf_op | source)
XLA Modules:
  0.0 28.4 jit_solution(14118023471429160008)
XLA Ops:
  1.3 1.4 %copy.7.quartet = s32[16,4]{1,0:T(8,128)} copy(s32[16,4]{0,1:T(4,128)} %param.8) | data formatting | bytes 512 | tf_op args[3]
  2.6 23.6 %build.1 = (f32[8,16,128]{2,1,0:T(8,128)}, f32[4,16,128]{2,1,0:T(8,128)}, s32[128]{0:T(128)}) custom-call(s32[16,4]{1,0:T(8,128)} %copy.7.quartet, s32[1]{0:T(128)S(6)} %copy.8.count, bf16[256,512]{1,0:T(8,128)(2,1)} %dens_a.1, bf16[256,512]{1,0:T(8,128)(2,1)} %dens_b.1, bf16[16,256,256]{2,1,0:T(8,128)(2,1)} %tiles.1), custom_call_target="tpu_custom_call" | custom-call | tf_op jit(solution)/shard_map/build/pallas_call | solution.py:364
  26.2 2.2 %place.1 = (f32[256,512]{1,0:T(8,128)}, f32[256,512]{1,0:T(8,128)}) custom-call(s32[128]{0:T(128)} %get-tuple-element.5.place, f32[8,16,128]{2,1,0:T(8,128)} %get-tuple-element.6.in_x, f32[4,16,128]{2,1,0:T(8,128)} %get-tuple-element.7.in_c), custom_call_target="tpu_custom_call" | custom-call | tf_op jit(solution)/shard_map/place/pallas_call | solution.py:404

commit v2 on v1

--- a/solution.py
+++ b/solution.py
@@ -35,16 +35,16 @@
 
 
 def build_kernel(
-    n_row, n_col, quartet, count, dens_a, dens_b, tiles,
+    n_row, n_col, hbm_quartet, hbm_count, hbm_a, hbm_b, tiles,
     out_x, out_c, place,
-    meta_c, meta_r, split_a, split_b, summed, held, send_c, recv_c, send_r, recv_r,
-    drep_a, drep_b, left_j, part_a, part_b, part_j,
+    quartet, count, dens_a, dens_b, meta_c, meta_r, split_a, split_b, summed, held, send_c, recv_c, send_r, recv_r,
+    drep_a, drep_b, weights, part_a, part_b, blocks_j,
     xs, xr, cs, cr,
-    tile_sem, sems_c, semr_c, sems_r, semr_r,
+    index_sem, dens_sem, tile_sem, sems_c, semr_c, sems_r, semr_r,
 ):
     slots, width = tiles.shape[0], tiles.shape[1]
-    row_blocks = dens_a.shape[0] // SHELL
-    col_blocks = dens_a.shape[1] // SHELL
+    row_blocks = hbm_a.shape[0] // SHELL
+    col_blocks = hbm_a.shape[1] // SHELL
     chunks = col_blocks // PACK
     row_cap, col_cap = slots // n_row, slots // n_col
     my_row, my_col = lax.axis_index("row"), lax.axis_index("col")
@@ -70,6 +70,18 @@
             device_id=(my_row, peer), device_id_type=MESH,
         )
 
+    index_copies = [
+        pltpu.make_async_copy(src, dst, index_sem.at[n])
+        for n, (src, dst) in enumerate(((hbm_quartet, quartet), (hbm_count, count)))
+    ]
+    for copy in index_copies:
+        copy.start()
+    dens_copies = [
+        pltpu.make_async_copy(src, dst, dens_sem.at[n])
+        for n, (src, dst) in enumerate(((hbm_a, dens_a), (hbm_b, dens_b)))
+    ]
+    for copy in dens_copies:
+        copy.start()
     barrier = pltpu.get_barrier_semaphore()
     for step in range(1, n_row):
         pl.semaphore_signal(
@@ -90,21 +102,26 @@
     for copy in tile_copies:
         copy.start()
 
+    for copy in index_copies:
+        copy.wait()
+
     live_count = count[0]
-    keys = [lax.div(quartet[t, 0], row_blocks) * slots + t for t in range(slots)]
+    keys = [lax.div(quartet[0, t], row_blocks) * slots + t for t in range(slots)]
 
     def pick(u, previous):
         found = [jnp.where(key > previous, key, 1 << 30) for key in keys]
         while len(found) > 1:
             found = [jnp.minimum(a, b) for a, b in zip(found[::2], found[1::2])]
         t = lax.rem(found[0], slots)
-        words = [quartet[t, n] for n in range(4)] + [jnp.where(t < live_count, 1, 0), t]
+        words = [quartet[n, t] for n in range(4)] + [jnp.where(t < live_count, 1, 0), t]
         for n, word in enumerate(words):
             meta_c[my_row, u * WORDS + n] = word
             meta_r[my_col, u * WORDS + n] = word
         return found[0]
 
     lax.fori_loop(0, slots, pick, jnp.int32(-1))
+    for copy in dens_copies:
+        copy.wait()
     for block_row in range(row_blocks):
         for chunk in range(chunks):
             rows = slice(block_row * SHELL, (block_row + 1) * SHELL)
@@ -204,14 +221,10 @@
     lax.fori_loop(0, n_col, place_col, 0)
 
     fold = one_hot((LANES, width), lambda i, j: lax.rem(i, SHELL) == lax.rem(j, SHELL))
-    spread = one_hot((LANES, width), lambda i, j: lax.rem(i, SHELL) == lax.div(j, SHELL))
     gather = one_hot((width, LANES), lambda i, j: lax.div(i, SHELL) == lax.rem(j, SHELL))
-    total_rows = slots * SHELL
-    same_slot = one_hot(
-        (total_rows, total_rows), lambda i, j: lax.div(i, SHELL) == lax.div(j, SHELL)
-    )
-    shape = (total_rows, width)
-    diagonal = lax.rem(iota(shape, 0), SHELL) == lax.rem(iota(shape, 1), SHELL)
+    pick_slot = [one_hot((LANES, LANES), lambda i, j: i // SHELL == slot) for slot in range(PACK)]
+    shape = (SHELL * SHELL, LANES)
+    own_r = iota(shape, 0) // SHELL == lax.rem(iota(shape, 1), SHELL)
 
     def expand(packed):
         return jnp.concatenate(
@@ -271,24 +284,23 @@
     xr[my_row] = xs[my_row]
 
     coul = arrive(n_row, column_copy, row_peer, recv_c)
-    left_j[...] = dot(
-        same_slot, jnp.where(diagonal, dot(expand(coul), spread), 0.0).astype(BF16)
-    ).astype(BF16)
+    for half in range(slots // PACK):
+        block = coul[half * SHELL : (half + 1) * SHELL]
+        stacked = jnp.concatenate([block] * SHELL, axis=0)
+        column = jnp.where(own_r, stacked, 0.0).astype(BF16)
+        for slot in range(PACK):
+            weights[half * PACK + slot] = dot(column, pick_slot[slot]).astype(BF16)
 
     def coulomb(t, carry):
-        rows = pl.ds(pl.multiple_of(t * SHELL, SHELL), SHELL)
-        part_j[rows, :] = lax.dot_general(
-            left_j[rows, :], held[meta_c[my_row, t * WORDS + 5]], (((1,), (1,)), ((), ())), preferred_element_type=F32
-        )
-        return carry
-
-    lax.fori_loop(0, slots, coulomb, 0)
-    coul_blocks = dot_split(jnp.where(diagonal, part_j[...], 0.0), gather)
+        out = dot(held[meta_c[my_row, t * WORDS + 5]], weights[t])
+        blocks_j[t] = jnp.sum(jnp.where(own_r, out, 0.0).reshape(SHELL, SHELL, LANES), axis=0)
+        return carry
+
+    lax.fori_loop(0, slots, coulomb, 0, unroll=4)
     for k in range(n_col):
         total = jnp.zeros((SHELL, LANES), F32)
         for m in range(col_cap):
-            first = (k * col_cap + m) * SHELL
-            total = jnp.where(group == m, coul_blocks[first : first + SHELL], total)
+            total = jnp.where(group == m, blocks_j[k * col_cap + m], total)
         cs[k] = total
 
     def send_j(step, carry):
@@ -357,6 +369,7 @@
     slots, width = integrals.shape[0], integrals.shape[1]
     vmem = pl.BlockSpec(memory_space=pltpu.VMEM)
     smem = pl.BlockSpec(memory_space=pltpu.SMEM)
+    hbm = pl.BlockSpec(memory_space=pltpu.HBM)
     rows = slots * SHELL
     pack_rows = slots // PACK * SHELL
     meta_words = max(LANES, slots * WORDS)
@@ -368,9 +381,13 @@
             jax.ShapeDtypeStruct((n_col, SHELL, LANES), F32),
             jax.ShapeDtypeStruct((slots * 8,), jnp.int32),
         ),
-        in_specs=[smem, smem, vmem, vmem, pl.BlockSpec(memory_space=pl.ANY)],
+        in_specs=[hbm] * 5,
         out_specs=(vmem, vmem, smem),
         scratch_shapes=[
+            pltpu.SMEM((4, slots), jnp.int32),
+            pltpu.SMEM((1,), jnp.int32),
+            pltpu.VMEM(dens_alpha.shape, BF16),
+            pltpu.VMEM(dens_alpha.shape, BF16),
             pltpu.SMEM((n_row, meta_words), jnp.int32),
             pltpu.SMEM((n_col, meta_words), jnp.int32),
             split,
@@ -383,14 +400,16 @@
             pltpu.VMEM((n_col, 2 * pack_rows, LANES), BF16),
             pltpu.VMEM((rows, width), F32),
             pltpu.VMEM((rows, width), F32),
-            pltpu.VMEM((rows, width), BF16),
+            pltpu.VMEM((slots, width, LANES), BF16),
             pltpu.VMEM((rows, width), F32),
             pltpu.VMEM((rows, width), F32),
-            pltpu.VMEM((rows, width), F32),
+            pltpu.VMEM((slots, SHELL, LANES), F32),
             pltpu.VMEM((n_row, SHELL, LANES), F32),
             pltpu.VMEM((n_row, SHELL, LANES), F32),
             pltpu.VMEM((n_col, SHELL, LANES), F32),
             pltpu.VMEM((n_col, SHELL, LANES), F32),
+            pltpu.SemaphoreType.DMA((2,)),
+            pltpu.SemaphoreType.DMA((2,)),
             pltpu.SemaphoreType.DMA((4,)),
             pltpu.SemaphoreType.DMA((3, n_row)),
             pltpu.SemaphoreType.DMA((3, n_row)),
@@ -399,7 +418,7 @@
         ],
         compiler_params=pltpu.CompilerParams(collective_id=0, has_side_effects=True),
         name="build",
-    )(tile_quartet, tile_count, dens_alpha, dens_beta, integrals)
+    )(tile_quartet.T, tile_count, dens_alpha, dens_beta, integrals)
     out = jax.ShapeDtypeStruct(dens_alpha.shape, F32)
     return pl.pallas_call(
         place_kernel,

time: 28.6 us -> 24.2 us (0.85)
  Pallas kernels: 25.7 us -> 22.8 us
  local copies, waits for them, and re-layouts: 1.36 us -> 0 us
    pallas_call x1, Pallas kernels: 23.6 us -> 20.6 us  [local(): pl.pallas_call(functools.partial(build_kernel, n_row, n_col), out_shape=(...]
    unnamed x1 -> x0, local copies, waits for them, and re-layouts: 1.36 us -> none
where the time goes in v2:
time: 24.2 us; the launch traced here: 24.1 us
  Pallas kernels  22.8 us (94%)
  between operations  1.29 us (5%)
    pallas_call x1, Pallas kernels, local(): pl.pallas_call(functools.partial(build_kernel, n_row, n_col), out_shape=(...  20.6 us
    pallas_call x1, Pallas kernels, local(): pl.pallas_call(place_kernel, out_shape=(out, out), in_specs=[smem, vmem,...  2.16 us

profile of v2, /device:TPU:0, one launch (start us, length us, event | category | flops | bytes accessed | tf_op | source)
XLA Modules:
  0.0 24.1 jit_solution(11447007653035814599)
XLA Ops:
  1.3 20.6 %build.1 = (f32[8,16,128]{2,1,0:T(8,128)}, f32[4,16,128]{2,1,0:T(8,128)}, s32[128]{0:T(128)}) custom-call(s32[4,16]{1,0:T(4,128)} %bitcast.1, s32[1]{0:T(128)S(6)} %copy.7.hbm_count, bf16[256,512]{1,0:T(8,128)(2,1)} %hbm_a.1, bf16[256,512]{1,0:T(8,128)(2,1)} %hbm_b.1, bf16[16,256,256]{2,1,0:T(8,128)(2,1)} %tiles.1), custom_call_target="tpu_custom_call" | custom-call | tf_op jit(solution)/shard_map/build/pallas_call | solution.py:377
  21.9 2.2 %place.1 = (f32[256,512]{1,0:T(8,128)}, f32[256,512]{1,0:T(8,128)}) custom-call(s32[128]{0:T(128)} %get-tuple-element.5.place, f32[8,16,128]{2,1,0:T(8,128)} %get-tuple-element.6.in_x, f32[4,16,128]{2,1,0:T(8,128)} %get-tuple-element.7.in_c), custom_call_target="tpu_custom_call" | custom-call | tf_op jit(solution)/shard_map/place/pallas_call | solution.py:423
